TPU v7x, 32 devices: a whole 2x2x4 slice. The times are simulated.
32 devices in a mesh: cells: 8 (over z, x), genes: 4 (over y, core).
Axes of the slice: x: 2, y: 2, z: 4, core: 2. Of those that a mesh axis runs over, the one named last changes fastest.
Arguments:
- expression: bfloat16 [32768, 4096], P('cells', 'genes'), may hold values from -200 to 200
- labels: int32 [32768], P('cells'), may hold values from 0 to 199, as said below
- loadings: bfloat16 [4096, 50], P('genes'), may hold values from -0.09375 to 0.09375
Outputs:
- adjusted: bfloat16 [32768, 4096], P('cells', 'genes')
- scores: float32 [32768, 50], P('cells')
Inputs may be any that keep to these rules, and one draw needn't show every extreme that they name: `labels`: every batch has two or more cells.
All inputs are finite; a program needn't handle non-finite values.
Results may differ from a plain program's by a relative error of at most 0.0029.
Values sent between devices are 32-bit elements; how exact they have to be, the bound alone decides.
No kernel may reach another device: no remote copies, remote signals or barrier semaphores. Data moves between devices by JAX's collectives and lax.ppermute only.
A program may use at most 64 MiB of HBM per device.

v0:
```python
import math
import jax
import jax.numpy as jnp
from jax import lax
from jax.sharding import PartitionSpec as P

GENES = 4096
BATCHES = 200
SWEEPS = 10


def batch_moments(sum_one, sum_two, counts, total_cells):
    grand = jnp.sum(sum_one, axis=0) / total_cells
    within = sum_two - sum_one * sum_one / counts[:, None]
    pooled = jnp.sum(within, axis=0) / total_cells + 1e-06
    gene_sd = jnp.sqrt(pooled)
    gamma_hat = (sum_one / counts[:, None] - grand[None, :]) / gene_sd[None, :]
    delta_hat = within / ((counts[:, None] - 1.0) * pooled[None, :])
    return (grand, gene_sd, gamma_hat, delta_hat)


def gene_terms(gamma_hat, delta_hat):
    return (
        jnp.sum(gamma_hat, axis=1),
        jnp.sum(gamma_hat * gamma_hat, axis=1),
        jnp.sum(delta_hat, axis=1),
        jnp.sum(delta_hat * delta_hat, axis=1),
    )


def shrink(gamma_hat, delta_hat, counts, spread):
    sum_gamma, sum_gamma_sq, sum_delta, sum_delta_sq = spread
    gamma_bar = sum_gamma / GENES
    tau_sq = (sum_gamma_sq - GENES * gamma_bar * gamma_bar) / (GENES - 1)
    delta_mean = sum_delta / GENES
    delta_var = (sum_delta_sq - GENES * delta_mean * delta_mean) / (GENES - 1) + 1e-06
    a_prior = (2.0 * delta_var + delta_mean * delta_mean) / delta_var
    b_prior = (delta_mean * delta_var + delta_mean**3) / delta_var
    weight = counts[:, None]

    def sweep(sweep_index, state):
        gamma_now, delta_now = state
        gamma_next = (weight * tau_sq[:, None] * gamma_hat + delta_now * gamma_bar[:, None]) / (
            weight * tau_sq[:, None] + delta_now
        )
        sum_sq = (weight - 1.0) * delta_hat + weight * (gamma_hat - gamma_next) ** 2
        delta_next = (0.5 * sum_sq + b_prior[:, None]) / (0.5 * weight + a_prior[:, None] - 1.0)
        return (gamma_next, delta_next)

    gamma_star, delta_star = lax.fori_loop(0, SWEEPS, sweep, (gamma_hat, delta_hat))
    return (gamma_star, 1.0 / jnp.sqrt(delta_star))


def split_three(initial):
    upper_part = lax.optimization_barrier(initial.astype(jnp.bfloat16))
    remainder = initial - upper_part.astype(jnp.float32)
    middle_part = lax.optimization_barrier(remainder.astype(jnp.bfloat16))
    lower_part = (remainder - middle_part.astype(jnp.float32)).astype(jnp.bfloat16)
    return (upper_part, middle_part, lower_part)


def body(expression, labels, loadings):
    cell_rows, gene_cols = expression.shape
    block_rows = math.gcd(cell_rows, 1024)
    block_count = cell_rows // block_rows
    indices = jnp.arange(block_count, dtype=jnp.int32)
    batch_ids = jnp.arange(BATCHES, dtype=jnp.int32)
    total_cells = cell_rows * lax.axis_size("cells")

    def members_of(start):
        local_labels = lax.dynamic_slice_in_dim(labels, start, block_rows, 0)
        return (batch_ids[:, None] == local_labels[None, :]).astype(jnp.bfloat16)

    def accumulate(totals, block_index):
        start = block_index * block_rows
        values = lax.dynamic_slice_in_dim(expression, start, block_rows, 0)
        widened = values.astype(jnp.float32)
        square_upper, square_middle, square_lower = split_three(widened * widened)
        stacked = jnp.concatenate([values, square_upper, square_middle, square_lower], axis=1)
        members = members_of(start)
        product = jnp.dot(members, stacked, preferred_element_type=jnp.float32)
        first = product[:, :gene_cols]
        second = (
            product[:, gene_cols : 2 * gene_cols]
            + product[:, 2 * gene_cols : 3 * gene_cols]
            + product[:, 3 * gene_cols :]
        )
        number = jnp.sum(members.astype(jnp.float32), axis=1)
        return ((totals[0] + first, totals[1] + second, totals[2] + number), None)

    zeros_table = jnp.zeros((BATCHES, gene_cols), jnp.float32)
    (sum_one, sum_two, counts), unused = lax.scan(
        accumulate, (zeros_table, zeros_table, jnp.zeros((BATCHES,), jnp.float32)), indices
    )
    sum_one, sum_two, counts = lax.psum((sum_one, sum_two, counts), "cells")
    grand, gene_sd, gamma_hat, delta_hat = batch_moments(sum_one, sum_two, counts, total_cells)
    spread = lax.psum(gene_terms(gamma_hat, delta_hat), "genes")
    gamma_star, scale_star = shrink(gamma_hat, delta_hat, counts, spread)
    table_parts = split_three(jnp.concatenate([gamma_star, scale_star], axis=1))

    def adjust(block_index):
        start = block_index * block_rows
        values = lax.dynamic_slice_in_dim(expression, start, block_rows, 0).astype(jnp.float32)
        members = members_of(start)
        looked = lax.dot_general(
            members, table_parts[0], (((0,), (0,)), ((), ())), preferred_element_type=jnp.float32
        )
        looked = looked + lax.dot_general(
            members, table_parts[1], (((0,), (0,)), ((), ())), preferred_element_type=jnp.float32
        )
        looked = looked + lax.dot_general(
            members, table_parts[2], (((0,), (0,)), ((), ())), preferred_element_type=jnp.float32
        )
        shifted = (values - grand[None, :]) / gene_sd[None, :]
        standard = (shifted - looked[:, :gene_cols]) * looked[:, gene_cols:]
        adjusted = (gene_sd[None, :] * standard + grand[None, :]).astype(jnp.bfloat16)
        standard_low = standard.astype(jnp.bfloat16)
        partial_value = jnp.dot(standard_low, loadings, preferred_element_type=jnp.float32)
        return (adjusted, partial_value)

    adjusted, partial_value = lax.map(adjust, indices)
    adjusted = adjusted.reshape(cell_rows, gene_cols)
    partial_value = partial_value.reshape(cell_rows, loadings.shape[1])
    scores = lax.psum(partial_value, "genes")
    return (adjusted, scores)


def solution(mesh):
    placed = (P("cells", "genes"), P("cells"), P("genes", None))
    return jax.shard_map(
        body,
        mesh=mesh,
        in_specs=placed,
        out_specs=(P("cells", "genes"), P("cells", None)),
        check_vma=False,
    )
```

profile of v0, /device:TPU:0, one launch (start us, length us, event | category | flops | bytes accessed | tf_op | source)
XLA Modules:
  0.0 286.7 jit_solution(8608671346428369143)
XLA Ops:
  7.2 47.7 %while.45 = (s32[]{:T(128)}, f32[200,1024]{1,0:T(8,128)}, f32[200,1024]{1,0:T(8,128)}, f32[200]{0:T(256)S(1)}, s32[4]{0:T(128)S(1)}, /*index=5*/s32[4096]{0:T(10...) while((s32[]{:T(128)}, f32[200,1024]{1,0:T(8,128)}, ...), condition=%wide.region_2.3_spmd.clone, body=%wide.region_0.2_spmd.clone.sunk | while | flops 1729257600 | bytes 39210296 | solution.py:92
  8.5 2.4 fusion.69
  12.0 1.6 subtract_convert_fusion.3
  14.2 2.0 fusion.71
  16.2 1.7 fusion.72
  19.4 2.4 fusion.69
  22.8 1.6 subtract_convert_fusion.3
  25.1 2.0 fusion.71
  27.1 3.1 %fusion.72 = (f32[200,1024]{1,0:T(8,128)}, f32[200,1024]{1,0:T(8,128)}) fusion(f32[200,4096]{1,0:T(8,128)S(1)} %fusion.71, f32[200,1024]{1,0:T(8,128)} %get-tuple-element.627, pred[]{:T(512)S(6)} %compare.3, f32[200,1024]{1,0:T(8,128)} %get-tuple-element.626), kind=kLoop, calls=%fused_computation.35.clone.1 | loop fusion | flops 1228800 | bytes 6553601 | tf_op jit(solution)/shard_map/while/body/eval_jaxpr/add | solution.py:89
  31.6 2.4 fusion.69
  37.4 2.0 fusion.71
  39.4 3.1 %fusion.72 = (f32[200,1024]{1,0:T(8,128)}, f32[200,1024]{1,0:T(8,128)}) fusion(f32[200,4096]{1,0:T(8,128)S(1)} %fusion.71, f32[200,1024]{1,0:T(8,128)} %get-tuple-element.627, pred[]{:T(512)S(6)} %compare.3, f32[200,1024]{1,0:T(8,128)} %get-tuple-element.626), kind=kLoop, calls=%fused_computation.35.clone.1 | loop fusion | flops 1228800 | bytes 6553601 | tf_op jit(solution)/shard_map/while/body/eval_jaxpr/add | solution.py:89
  43.9 2.4 fusion.69
  49.6 2.0 fusion.71
  51.6 3.1 %fusion.72 = (f32[200,1024]{1,0:T(8,128)}, f32[200,1024]{1,0:T(8,128)}) fusion(f32[200,4096]{1,0:T(8,128)S(1)} %fusion.71, f32[200,1024]{1,0:T(8,128)} %get-tuple-element.627, pred[]{:T(512)S(6)} %compare.3, f32[200,1024]{1,0:T(8,128)} %get-tuple-element.626), kind=kLoop, calls=%fused_computation.35.clone.1 | loop fusion | flops 1228800 | bytes 6553601 | tf_op jit(solution)/shard_map/while/body/eval_jaxpr/add | solution.py:89
  55.0 23.9 %psum.58 = f32[200]{0:T(256)S(1)} all-reduce(f32[200]{0:T(256)S(1)} %get-tuple-element.268), channel_id=1, replica_groups=mesh['cells'=8,'genes'=4] {'cells'}, use_global_device_ids=true, to_apply=%region_4.5 | all-reduce | flops 200 | bytes 1600 | tf_op jit(solution)/shard_map/psum | solution.py:95
  78.9 70.5 %all-reduce.7.cloned.1.call-done = (f32[200,1024]{1,0:T(8,128)}, f32[200,1024]{1,0:T(8,128)}) async-done(((f32[200,1024]{1,0:T(8,128)}, f32[200,1024]{1,0:T(8,128)}), (f32[200,1024]{1,0:T(8,128)}, f32[200,1024]{1,0:T(8,128)})) %all-reduce.7.cloned.1.call-update) | async-done | bytes 1638416 | tf_op jit(solution)/shard_map/psum | solution.py:95
  149.5 1.6 fusion.39
  151.1 2.0 multiply_reduce_fusion
  154.1 7.0 %all-reduce.1 = (f32[200]{0:T(256)S(1)}, f32[200]{0:T(256)S(1)}, f32[200]{0:T(256)S(1)}, f32[200]{0:T(256)S(1)}) all-reduce(f32[200]{0:T(256)S(1)} %get-tuple-element.407, f32[200]{0:T(256)S(1)} %get-tuple-element.408, f32[200]{0:T(256)S(1)} %get-tuple-element.326, ...), channel_id=1, replica_groups=mesh['cells'=8,'genes'=4] {'genes'}, use_global_device_ids=true, to_apply=%region_15.16 | all-reduce | flops 800 | bytes 6400 | tf_op jit(solution)/shard_map/psum | solution.py:97
  161.1 13.3 %while.43 = (s32[]{:T(128)}, f32[200,1024]{1,0:T(8,128)}, f32[200,1024]{1,0:T(8,128)S(1)}, f32[200,1]{0,1:T(1,128)S(1)}, f32[200,1024]{1,0:T(8,128)S(1)}, /*inde...) while((s32[]{:T(128)}, f32[200,1024]{1,0:T(8,128)}, ...), condition=%wide.region_17.18_spmd, body=%wide.region_16.17_spmd.sunk | while | flops 2663202 | bytes 4104109 | solution.py:50
  176.8 63.9 %while.44 = (s32[]{:T(128)}, bf16[4,1024,1024]{2,1,0:T(8,128)(2,1)}, f32[4,1024,50]{1,0,2:T(4,128)}, f32[1024]{0:T(1024)S(1)}, s32[4]{0:T(128)S(1)}, /*index=5*/...) while((s32[]{:T(128)}, ...), condition=%wide.region_19.20_spmd.clone, body=%wide.region_18.19_spmd.clone.sunk | while | flops 2635685888 | bytes 62333656 | solution.py:121
  183.0 3.7 %fusion.66 = (bf16[4,1024,1024]{2,1,0:T(8,128)(2,1)}, bf16[1024,1024]{1,0:T(8,128)(2,1)S(1)}) fusion(bf16[4,1024,1024]{2,1,0:T(8,128)(2,1)} %get-tuple-element.697, s32[]{:T(128)} %get-tuple-element.696, f32[1024]{0:T(1024)S(1)} %get-tuple-element.718, f32[1024]{0:T(1024)S(1)} %get-tuple-element.715, f32[1024,2048]{1,0:T(8,128)S(1)} %add_add_fusion.3, ...), kind=kLoop, calls=%fused_computation.11.clone.1 | loop fusion | flops 9437184 | bytes 14688772 | tf_op jit(solution)/shard_map/while/body/jit(dynamic_update_index_in_dim)/dynamic_update_slice | solution.py:121
  187.7 5.1 %dynamic_update_slice.14 = f32[4,1024,50]{1,0,2:T(4,128)} dynamic-update-slice(f32[4,1024,50]{1,0,2:T(4,128)} %get-tuple-element.698, f32[1,1024,50]{1,0,2:T(1,128)S(1)} %copy.17, s32[]{:T(128)} %get-tuple-element.696, s32[]{:T(128)} %constant.76.clone.1..sunk, s32[]{:T(128)} %constant.76.clone.1..sunk) | dynamic-update-slice | bytes 409604 | tf_op jit(solution)/shard_map/while/body/jit(dynamic_update_index_in_dim)/dynamic_update_slice | solution.py:121
  199.0 3.7 %fusion.66 = (bf16[4,1024,1024]{2,1,0:T(8,128)(2,1)}, bf16[1024,1024]{1,0:T(8,128)(2,1)S(1)}) fusion(bf16[4,1024,1024]{2,1,0:T(8,128)(2,1)} %get-tuple-element.697, s32[]{:T(128)} %get-tuple-element.696, f32[1024]{0:T(1024)S(1)} %get-tuple-element.718, f32[1024]{0:T(1024)S(1)} %get-tuple-element.715, f32[1024,2048]{1,0:T(8,128)S(1)} %add_add_fusion.3, ...), kind=kLoop, calls=%fused_computation.11.clone.1 | loop fusion | flops 9437184 | bytes 14688772 | tf_op jit(solution)/shard_map/while/body/jit(dynamic_update_index_in_dim)/dynamic_update_slice | solution.py:121
  203.7 5.1 %dynamic_update_slice.14 = f32[4,1024,50]{1,0,2:T(4,128)} dynamic-update-slice(f32[4,1024,50]{1,0,2:T(4,128)} %get-tuple-element.698, f32[1,1024,50]{1,0,2:T(1,128)S(1)} %copy.17, s32[]{:T(128)} %get-tuple-element.696, s32[]{:T(128)} %constant.76.clone.1..sunk, s32[]{:T(128)} %constant.76.clone.1..sunk) | dynamic-update-slice | bytes 409604 | tf_op jit(solution)/shard_map/while/body/jit(dynamic_update_index_in_dim)/dynamic_update_slice | solution.py:121
  214.9 3.7 %fusion.66 = (bf16[4,1024,1024]{2,1,0:T(8,128)(2,1)}, bf16[1024,1024]{1,0:T(8,128)(2,1)S(1)}) fusion(bf16[4,1024,1024]{2,1,0:T(8,128)(2,1)} %get-tuple-element.697, s32[]{:T(128)} %get-tuple-element.696, f32[1024]{0:T(1024)S(1)} %get-tuple-element.718, f32[1024]{0:T(1024)S(1)} %get-tuple-element.715, f32[1024,2048]{1,0:T(8,128)S(1)} %add_add_fusion.3, ...), kind=kLoop, calls=%fused_computation.11.clone.1 | loop fusion | flops 9437184 | bytes 14688772 | tf_op jit(solution)/shard_map/while/body/jit(dynamic_update_index_in_dim)/dynamic_update_slice | solution.py:121
  219.6 5.1 %dynamic_update_slice.14 = f32[4,1024,50]{1,0,2:T(4,128)} dynamic-update-slice(f32[4,1024,50]{1,0,2:T(4,128)} %get-tuple-element.698, f32[1,1024,50]{1,0,2:T(1,128)S(1)} %copy.17, s32[]{:T(128)} %get-tuple-element.696, s32[]{:T(128)} %constant.76.clone.1..sunk, s32[]{:T(128)} %constant.76.clone.1..sunk) | dynamic-update-slice | bytes 409604 | tf_op jit(solution)/shard_map/while/body/jit(dynamic_update_index_in_dim)/dynamic_update_slice | solution.py:121
  230.9 3.7 %fusion.66 = (bf16[4,1024,1024]{2,1,0:T(8,128)(2,1)}, bf16[1024,1024]{1,0:T(8,128)(2,1)S(1)}) fusion(bf16[4,1024,1024]{2,1,0:T(8,128)(2,1)} %get-tuple-element.697, s32[]{:T(128)} %get-tuple-element.696, f32[1024]{0:T(1024)S(1)} %get-tuple-element.718, f32[1024]{0:T(1024)S(1)} %get-tuple-element.715, f32[1024,2048]{1,0:T(8,128)S(1)} %add_add_fusion.3, ...), kind=kLoop, calls=%fused_computation.11.clone.1 | loop fusion | flops 9437184 | bytes 14688772 | tf_op jit(solution)/shard_map/while/body/jit(dynamic_update_index_in_dim)/dynamic_update_slice | solution.py:121
  235.6 5.1 %dynamic_update_slice.14 = f32[4,1024,50]{1,0,2:T(4,128)} dynamic-update-slice(f32[4,1024,50]{1,0,2:T(4,128)} %get-tuple-element.698, f32[1,1024,50]{1,0,2:T(1,128)S(1)} %copy.17, s32[]{:T(128)} %get-tuple-element.696, s32[]{:T(128)} %constant.76.clone.1..sunk, s32[]{:T(128)} %constant.76.clone.1..sunk) | dynamic-update-slice | bytes 409604 | tf_op jit(solution)/shard_map/while/body/jit(dynamic_update_index_in_dim)/dynamic_update_slice | solution.py:121
  243.5 34.2 %all-reduce.5.cloned.1.call-done = f32[4096,50]{0,1:T(8,128)} async-done(((f32[4096,50]{0,1:T(8,128)}), f32[4096,50]{0,1:T(8,128)}) %all-reduce.5.cloned.1.call-update) | async-done | bytes 819216 | tf_op jit(solution)/shard_map/psum | solution.py:124
  277.7 2.2 copy.53
  (97 shorter events, 58.3 us)
Async XLA Ops:
  7.2 142.3 %all-reduce.7.cloned.1.call-start = ((), (), s32[]{:S(2)}) async-start(), calls=%async_computation.1 | async-start | bytes 3276800 | tf_op jit(solution)/shard_map/psum | solution.py:95
  54.9 222.7 %all-reduce.5.cloned.1.call-start = ((), (), s32[]{:S(2)}) async-start(), calls=%async_computation | async-start | bytes 1835008 | tf_op jit(solution)/shard_map/psum | solution.py:124
  174.4 1.4 copy-start
  175.9 0.9 copy-start.1
Sparse Core Ops, SparseCore 0:
  55.1 94.3 all-reduce.6
  243.6 34.0 all-reduce.4
where the time goes:
time: 288 us; the launch traced here: 287 us
  waiting for transfers between devices  105 us (36%)
  other arithmetic  65.5 us (23%)
  local copies, waits for them, and re-layouts  38 us (13%)
  blocking collectives  30.9 us (11%)
  matrix products  27.6 us (10%)
  between operations  14.2 us (5%)
  loops' own time  5.76 us (2%)
    psum x1, waiting for transfers between devices, body(): sum_one, sum_two, counts = lax.psum((sum_one, sum_two, counts), 'cells')  70.5 us
    psum x1, waiting for transfers between devices, body(): scores = lax.psum(partial_value, 'genes')  34.2 us
    psum x1, blocking collectives, body(): sum_one, sum_two, counts = lax.psum((sum_one, sum_two, counts), 'cells')  23.9 us
    dynamic_update_slice x8, local copies, waits for them, and re-layouts, body(): adjusted, partial_value = lax.map(adjust, indices)  21.1 us
    dynamic_update_slice x4, other arithmetic, body(): adjusted, partial_value = lax.map(adjust, indices)  14.9 us
    div x10, other arithmetic, sweep(): (0.5 * sum_sq + b_prior[:, None]) / (0.5 * weight + a_prior[:, None] - 1.0)  13.2 us
    convert_element_type x5, other arithmetic, split_three(): upper_part = lax.optimization_barrier(initial.astype(jnp.bfloat16))  11.1 us
    add x8, other arithmetic, accumulate(): return ((totals[0] + first, totals[1] + second, totals[2] + number), None)  11 us
  transfers between devices with their start and end apart: 2, of which 2 were waited for; matrix products, arithmetic and copies ran while one was open for 0% of the time, Pallas kernels for 0%

commit v1 on v0

--- a/solution.py
+++ b/solution.py
@@ -7,6 +7,14 @@
 GENES = 4096
 BATCHES = 200
 SWEEPS = 10
+
+
+def add_in_pairs(x, axis):
+    size, total = (lax.axis_size(axis), x)
+    for hop in [1 << k for k in range(size.bit_length() - 1)]:
+        route = [(i, i ^ hop) for i in range(size)]
+        total = total + lax.ppermute(total, axis, route)
+    return total
 
 
 def batch_moments(sum_one, sum_two, counts, total_cells):
@@ -121,7 +129,7 @@
     adjusted, partial_value = lax.map(adjust, indices)
     adjusted = adjusted.reshape(cell_rows, gene_cols)
     partial_value = partial_value.reshape(cell_rows, loadings.shape[1])
-    scores = lax.psum(partial_value, "genes")
+    scores = add_in_pairs(partial_value, "genes")
     return (adjusted, scores)
 
 

time: 288 us -> 277 us (0.962)
  waiting for transfers between devices: 105 us -> 95 us
  local copies, waits for them, and re-layouts: 38 us -> 34.9 us
    psum x1 -> x0, waiting for transfers between devices: 34.2 us -> none  [body(): scores = lax.psum(partial_value, 'genes')]
    ppermute x0 -> x2, waiting for transfers between devices: none -> 24.3 us  [add_in_pairs(): total = total + lax.ppermute(total, axis, route)]
    unnamed x9 -> x8, local copies, waits for them, and re-layouts: 6.15 us -> 3.07 us
  transfers between devices with their start and end apart: 2 -> 3, of which waited for: 2 -> 3; matrix products, arithmetic and copies ran while one was open for 0% -> 0% of each run, Pallas kernels for 0% -> 0%
where the time goes in v1:
time: 277 us; the launch traced here: 276 us
  waiting for transfers between devices  95 us (34%)
  other arithmetic  66.6 us (24%)
  local copies, waits for them, and re-layouts  34.9 us (13%)
  blocking collectives  30.9 us (11%)
  matrix products  27.6 us (10%)
  between operations  14.2 us (5%)
  loops' own time  5.76 us (2%)
    psum x1, waiting for transfers between devices, body(): sum_one, sum_two, counts = lax.psum((sum_one, sum_two, counts), 'cells')  70.7 us
    ppermute x2, waiting for transfers between devices, add_in_pairs(): total = total + lax.ppermute(total, axis, route)  24.3 us
    psum x1, blocking collectives, body(): sum_one, sum_two, counts = lax.psum((sum_one, sum_two, counts), 'cells')  23.8 us
    dynamic_update_slice x8, local copies, waits for them, and re-layouts, body(): adjusted, partial_value = lax.map(adjust, indices)  21.1 us
    dynamic_update_slice x4, other arithmetic, body(): adjusted, partial_value = lax.map(adjust, indices)  14.9 us
    div x10, other arithmetic, sweep(): (0.5 * sum_sq + b_prior[:, None]) / (0.5 * weight + a_prior[:, None] - 1.0)  13.2 us
    convert_element_type x5, other arithmetic, split_three(): upper_part = lax.optimization_barrier(initial.astype(jnp.bfloat16))  11.1 us
    add x8, other arithmetic, accumulate(): return ((totals[0] + first, totals[1] + second, totals[2] + number), None)  11 us
  transfers between devices with their start and end apart: 3, of which 3 were waited for; matrix products, arithmetic and copies ran while one was open for 0% of the time, Pallas kernels for 0%

profile of v1, /device:TPU:0, one launch (start us, length us, event | category | flops | bytes accessed | tf_op | source)
XLA Modules:
  0.0 275.5 jit_solution(4019044979243054919)
XLA Ops:
  7.2 47.7 %while.45 = (s32[]{:T(128)}, f32[200,1024]{1,0:T(8,128)}, f32[200,1024]{1,0:T(8,128)}, f32[200]{0:T(256)S(1)}, s32[4]{0:T(128)S(1)}, /*index=5*/s32[4096]{0:T(10...) while((s32[]{:T(128)}, f32[200,1024]{1,0:T(8,128)}, ...), condition=%wide.region_2.3_spmd.clone, body=%wide.region_0.2_spmd.clone.sunk | while | flops 1729257600 | bytes 39210296 | solution.py:100
  8.5 2.4 fusion.69
  12.0 1.6 subtract_convert_fusion.3
  14.2 2.0 fusion.71
  16.2 1.7 fusion.72
  19.4 2.4 fusion.69
  22.8 1.6 subtract_convert_fusion.3
  25.1 2.0 fusion.71
  27.1 3.1 %fusion.72 = (f32[200,1024]{1,0:T(8,128)}, f32[200,1024]{1,0:T(8,128)}) fusion(f32[200,4096]{1,0:T(8,128)S(1)} %fusion.71, f32[200,1024]{1,0:T(8,128)} %get-tuple-element.627, pred[]{:T(512)S(6)} %compare.3, f32[200,1024]{1,0:T(8,128)} %get-tuple-element.626), kind=kLoop, calls=%fused_computation.35.clone.1 | loop fusion | flops 1228800 | bytes 6553601 | tf_op jit(solution)/shard_map/while/body/eval_jaxpr/add | solution.py:97
  31.6 2.4 fusion.69
  37.4 2.0 fusion.71
  39.4 3.1 %fusion.72 = (f32[200,1024]{1,0:T(8,128)}, f32[200,1024]{1,0:T(8,128)}) fusion(f32[200,4096]{1,0:T(8,128)S(1)} %fusion.71, f32[200,1024]{1,0:T(8,128)} %get-tuple-element.627, pred[]{:T(512)S(6)} %compare.3, f32[200,1024]{1,0:T(8,128)} %get-tuple-element.626), kind=kLoop, calls=%fused_computation.35.clone.1 | loop fusion | flops 1228800 | bytes 6553601 | tf_op jit(solution)/shard_map/while/body/eval_jaxpr/add | solution.py:97
  43.9 2.4 fusion.69
  49.6 2.0 fusion.71
  51.6 3.1 %fusion.72 = (f32[200,1024]{1,0:T(8,128)}, f32[200,1024]{1,0:T(8,128)}) fusion(f32[200,4096]{1,0:T(8,128)S(1)} %fusion.71, f32[200,1024]{1,0:T(8,128)} %get-tuple-element.627, pred[]{:T(512)S(6)} %compare.3, f32[200,1024]{1,0:T(8,128)} %get-tuple-element.626), kind=kLoop, calls=%fused_computation.35.clone.1 | loop fusion | flops 1228800 | bytes 6553601 | tf_op jit(solution)/shard_map/while/body/eval_jaxpr/add | solution.py:97
  55.0 23.8 %psum.51 = f32[200]{0:T(256)S(1)} all-reduce(f32[200]{0:T(256)S(1)} %get-tuple-element.268), channel_id=1, replica_groups=mesh['cells'=8,'genes'=4] {'cells'}, use_global_device_ids=true, to_apply=%region_4.5 | all-reduce | flops 200 | bytes 1600 | tf_op jit(solution)/shard_map/psum | solution.py:103
  78.8 70.7 %all-reduce.4.cloned.1.call-done = (f32[200,1024]{1,0:T(8,128)}, f32[200,1024]{1,0:T(8,128)}) async-done(((f32[200,1024]{1,0:T(8,128)}, f32[200,1024]{1,0:T(8,128)}), (f32[200,1024]{1,0:T(8,128)}, f32[200,1024]{1,0:T(8,128)})) %all-reduce.4.cloned.1.call-update) | async-done | bytes 1638416 | tf_op jit(solution)/shard_map/psum | solution.py:103
  149.5 1.6 fusion.39
  151.1 2.0 multiply_reduce_fusion
  154.1 7.0 %all-reduce.1 = (f32[200]{0:T(256)S(1)}, f32[200]{0:T(256)S(1)}, f32[200]{0:T(256)S(1)}, f32[200]{0:T(256)S(1)}) all-reduce(f32[200]{0:T(256)S(1)} %get-tuple-element.407, f32[200]{0:T(256)S(1)} %get-tuple-element.408, f32[200]{0:T(256)S(1)} %get-tuple-element.326, ...), channel_id=1, replica_groups=mesh['cells'=8,'genes'=4] {'genes'}, use_global_device_ids=true, to_apply=%region_15.16 | all-reduce | flops 800 | bytes 6400 | tf_op jit(solution)/shard_map/psum | solution.py:105
  161.1 13.3 %while.43 = (s32[]{:T(128)}, f32[200,1024]{1,0:T(8,128)}, f32[200,1024]{1,0:T(8,128)S(1)}, f32[200,1]{0,1:T(1,128)S(1)}, f32[200,1024]{1,0:T(8,128)S(1)}, /*inde...) while((s32[]{:T(128)}, f32[200,1024]{1,0:T(8,128)}, ...), condition=%wide.region_17.18_spmd, body=%wide.region_16.17_spmd.sunk | while | flops 2663202 | bytes 4104109 | solution.py:58
  176.8 63.9 %while.44 = (s32[]{:T(128)}, bf16[4,1024,1024]{2,1,0:T(8,128)(2,1)}, f32[4,1024,50]{1,0,2:T(4,128)}, f32[1024]{0:T(1024)S(1)}, s32[4]{0:T(128)S(1)}, /*index=5*/...) while((s32[]{:T(128)}, ...), condition=%wide.region_19.20_spmd.clone, body=%wide.region_18.19_spmd.clone.sunk | while | flops 2635685888 | bytes 62333656 | solution.py:129
  183.0 3.7 %fusion.66 = (bf16[4,1024,1024]{2,1,0:T(8,128)(2,1)}, bf16[1024,1024]{1,0:T(8,128)(2,1)S(1)}) fusion(bf16[4,1024,1024]{2,1,0:T(8,128)(2,1)} %get-tuple-element.697, s32[]{:T(128)} %get-tuple-element.696, f32[1024]{0:T(1024)S(1)} %get-tuple-element.718, f32[1024]{0:T(1024)S(1)} %get-tuple-element.715, f32[1024,2048]{1,0:T(8,128)S(1)} %add_add_fusion.3, ...), kind=kLoop, calls=%fused_computation.11.clone.1 | loop fusion | flops 9437184 | bytes 14688772 | tf_op jit(solution)/shard_map/while/body/jit(dynamic_update_index_in_dim)/dynamic_update_slice | solution.py:129
  187.7 5.1 %dynamic_update_slice.14 = f32[4,1024,50]{1,0,2:T(4,128)} dynamic-update-slice(f32[4,1024,50]{1,0,2:T(4,128)} %get-tuple-element.698, f32[1,1024,50]{1,0,2:T(1,128)S(1)} %copy.17, s32[]{:T(128)} %get-tuple-element.696, s32[]{:T(128)} %constant.76.clone.1..sunk, s32[]{:T(128)} %constant.76.clone.1..sunk) | dynamic-update-slice | bytes 409604 | tf_op jit(solution)/shard_map/while/body/jit(dynamic_update_index_in_dim)/dynamic_update_slice | solution.py:129
  199.0 3.7 %fusion.66 = (bf16[4,1024,1024]{2,1,0:T(8,128)(2,1)}, bf16[1024,1024]{1,0:T(8,128)(2,1)S(1)}) fusion(bf16[4,1024,1024]{2,1,0:T(8,128)(2,1)} %get-tuple-element.697, s32[]{:T(128)} %get-tuple-element.696, f32[1024]{0:T(1024)S(1)} %get-tuple-element.718, f32[1024]{0:T(1024)S(1)} %get-tuple-element.715, f32[1024,2048]{1,0:T(8,128)S(1)} %add_add_fusion.3, ...), kind=kLoop, calls=%fused_computation.11.clone.1 | loop fusion | flops 9437184 | bytes 14688772 | tf_op jit(solution)/shard_map/while/body/jit(dynamic_update_index_in_dim)/dynamic_update_slice | solution.py:129
  203.7 5.1 %dynamic_update_slice.14 = f32[4,1024,50]{1,0,2:T(4,128)} dynamic-update-slice(f32[4,1024,50]{1,0,2:T(4,128)} %get-tuple-element.698, f32[1,1024,50]{1,0,2:T(1,128)S(1)} %copy.17, s32[]{:T(128)} %get-tuple-element.696, s32[]{:T(128)} %constant.76.clone.1..sunk, s32[]{:T(128)} %constant.76.clone.1..sunk) | dynamic-update-slice | bytes 409604 | tf_op jit(solution)/shard_map/while/body/jit(dynamic_update_index_in_dim)/dynamic_update_slice | solution.py:129
  214.9 3.7 %fusion.66 = (bf16[4,1024,1024]{2,1,0:T(8,128)(2,1)}, bf16[1024,1024]{1,0:T(8,128)(2,1)S(1)}) fusion(bf16[4,1024,1024]{2,1,0:T(8,128)(2,1)} %get-tuple-element.697, s32[]{:T(128)} %get-tuple-element.696, f32[1024]{0:T(1024)S(1)} %get-tuple-element.718, f32[1024]{0:T(1024)S(1)} %get-tuple-element.715, f32[1024,2048]{1,0:T(8,128)S(1)} %add_add_fusion.3, ...), kind=kLoop, calls=%fused_computation.11.clone.1 | loop fusion | flops 9437184 | bytes 14688772 | tf_op jit(solution)/shard_map/while/body/jit(dynamic_update_index_in_dim)/dynamic_update_slice | solution.py:129
  219.6 5.1 %dynamic_update_slice.14 = f32[4,1024,50]{1,0,2:T(4,128)} dynamic-update-slice(f32[4,1024,50]{1,0,2:T(4,128)} %get-tuple-element.698, f32[1,1024,50]{1,0,2:T(1,128)S(1)} %copy.17, s32[]{:T(128)} %get-tuple-element.696, s32[]{:T(128)} %constant.76.clone.1..sunk, s32[]{:T(128)} %constant.76.clone.1..sunk) | dynamic-update-slice | bytes 409604 | tf_op jit(solution)/shard_map/while/body/jit(dynamic_update_index_in_dim)/dynamic_update_slice | solution.py:129
  230.9 3.7 %fusion.66 = (bf16[4,1024,1024]{2,1,0:T(8,128)(2,1)}, bf16[1024,1024]{1,0:T(8,128)(2,1)S(1)}) fusion(bf16[4,1024,1024]{2,1,0:T(8,128)(2,1)} %get-tuple-element.697, s32[]{:T(128)} %get-tuple-element.696, f32[1024]{0:T(1024)S(1)} %get-tuple-element.718, f32[1024]{0:T(1024)S(1)} %get-tuple-element.715, f32[1024,2048]{1,0:T(8,128)S(1)} %add_add_fusion.3, ...), kind=kLoop, calls=%fused_computation.11.clone.1 | loop fusion | flops 9437184 | bytes 14688772 | tf_op jit(solution)/shard_map/while/body/jit(dynamic_update_index_in_dim)/dynamic_update_slice | solution.py:129
  235.6 5.1 %dynamic_update_slice.14 = f32[4,1024,50]{1,0,2:T(4,128)} dynamic-update-slice(f32[4,1024,50]{1,0,2:T(4,128)} %get-tuple-element.698, f32[1,1024,50]{1,0,2:T(1,128)S(1)} %copy.17, s32[]{:T(128)} %get-tuple-element.696, s32[]{:T(128)} %constant.76.clone.1..sunk, s32[]{:T(128)} %constant.76.clone.1..sunk) | dynamic-update-slice | bytes 409604 | tf_op jit(solution)/shard_map/while/body/jit(dynamic_update_index_in_dim)/dynamic_update_slice | solution.py:129
  242.6 2.5 collective-permute-done
  245.8 21.8 %collective-permute-done.1 = f32[4096,50]{0,1:T(8,128)S(1)} collective-permute-done((f32[4096,50]{0,1:T(8,128)S(1)}, f32[4096,50]{0,1:T(8,128)S(1)}, u32[]{:S(2)}, u32[]{:S(2)}) %collective-permute-start.1) | collective-permute-done | bytes 819232 | tf_op jit(solution)/shard_map/ppermute | solution.py:16
  (99 shorter events, 59.1 us)
Async XLA Ops:
  7.2 142.3 %all-reduce.4.cloned.1.call-start = ((), (), s32[]{:S(2)}) async-start(), calls=%async_computation | async-start | bytes 3276800 | tf_op jit(solution)/shard_map/psum | solution.py:103
  174.4 1.4 copy-start
  175.9 0.9 copy-start.1
  242.6 2.5 collective-permute-start
  245.2 22.5 %collective-permute-start.1 = (f32[4096,50]{0,1:T(8,128)S(1)}, f32[4096,50]{0,1:T(8,128)S(1)}, u32[]{:S(2)}, u32[]{:S(2)}) collective-permute-start(f32[4096,50]{0,1:T(8,128)S(1)} %add.173), channel_id=1, source_target_pairs={{0,2},{1,3},{2,0},{3,1},{4,6},{5,7},{6,4},{7,5},{8,10},{9,11},{10,... | collective-permute-start | bytes 2457608 | tf_op jit(solution)/shard_map/ppermute | solution.py:16
Sparse Core Ops, SparseCore 0:
  55.1 94.3 all-reduce.3
